TPU v7x, 32 devices: a whole 2x2x4 slice. The times are simulated.
32 devices in a mesh: groups: 2 (over y), seq: 8 (over z, x), sub: 2 (over core).
Axes of the slice: x: 2, y: 2, z: 4, core: 2. Of those that a mesh axis runs over, the one named last changes fastest.
Arguments:
- cache_in: bfloat16 [64, 2, 36864], P('groups', None, ('sub', 'seq')), parts along dimension 0, may hold values from -6 to 6
- page_counts: int32 [16], P('groups'), parts along dimension 0, may hold values from 1 to 8, 32 in all
- tail_tokens: int32 [16], P('groups'), parts along dimension 0, may hold values from 1 to 64
- assignment: int32 [16], P('groups'), parts along dimension 0, may hold values from 0 to 7, each once
Outputs:
- cache_out: bfloat16 [128, 2, 36864], P(('groups', 'seq'), None, 'sub'), parts along dimension 0
- checksum: float32 [2, 128], P(None, ('groups', 'seq')), parts along dimension 1
There are 2 independent parts, one for each index of `groups`. A program takes and returns all parts, laid end to end along the dimension named above; each array names one. Nothing has to cross between parts.
Inputs may be any that keep to these rules, and one draw needn't show every extreme that they name: `page_counts`: the page counts sum to 32. `assignment`: every seq index serves exactly one request.
All inputs are finite; a program needn't handle non-finite values.
Results may differ from a plain program's by a relative error of at most 0.001.
Values may be sent and summed in bfloat16 or wider, within the bound.
A program may use at most 64 MiB of HBM per device.

v0:
```python
import jax
import jax.numpy as jnp
from jax import lax
from jax.sharding import PartitionSpec as P

LATENT = 576
PAGE = 64
MAXP = 8


def by_device(matches, values):
    return jnp.sum(jnp.where(matches, values[None, :], 0), axis=1)


def shards(cache_in, page_counts, tail_tokens, assignment):
    seq_count = lax.axis_size("seq")
    own_index = lax.axis_index("seq")
    sub_index = lax.axis_index("sub")
    total_pages, layer_count, piece = cache_in.shape
    starts = jnp.cumsum(page_counts) - page_counts
    device_ids = jnp.arange(seq_count, dtype=jnp.int32)
    matches = assignment[None, :] == device_ids[:, None]
    dest_counts = by_device(matches, page_counts)
    dest_starts = by_device(matches, starts)
    dest_tails = by_device(matches, tail_tokens)
    slot_ids = jnp.arange(seq_count * MAXP, dtype=jnp.int32)
    page_rank = slot_ids % MAXP
    counts_at = jnp.repeat(dest_counts, MAXP)
    starts_at = jnp.repeat(dest_starts, MAXP)
    tails_at = jnp.repeat(dest_tails, MAXP)
    in_use = page_rank < counts_at
    source_rows = jnp.where(in_use, starts_at + page_rank, 0)
    filled = jnp.where(in_use, jnp.where(page_rank < counts_at - 1, PAGE, tails_at), 0)
    column = (sub_index * seq_count + own_index) * piece + jnp.arange(piece, dtype=jnp.int32)
    token_of = column // LATENT
    kept_mask = token_of[None, :] < filled[:, None]
    zero_value = jnp.zeros((), cache_in.dtype)
    fetched = jnp.take(cache_in, source_rows, axis=0)
    packed = jnp.where(kept_mask[:, None, :], fetched, zero_value)
    cache_out = lax.all_to_all(packed, "seq", split_axis=0, concat_axis=2, tiled=True)
    squares = jnp.sum(jnp.square(cache_out.astype(jnp.float32)), axis=2)
    squares = lax.psum(squares, "sub")
    checksum = jnp.sqrt(1.0 + squares / (PAGE * LATENT)).T
    return (cache_out, checksum)


def solution(mesh):
    placed = (P("groups", None, ("sub", "seq")), P("groups"), P("groups"), P("groups"))
    return jax.shard_map(
        shards,
        mesh=mesh,
        in_specs=placed,
        out_specs=(P(("groups", "seq"), None, "sub"), P(None, ("groups", "seq"))),
        check_vma=False,
    )
```

profile of v0, /device:TPU:0, one launch (start us, length us, event | category | flops | bytes accessed | tf_op | source)
XLA Modules:
  0.0 35.1 jit_solution(7010755200806696624)
XLA Ops:
  0.6 0.0 copy-start
  0.6 0.9 %reduce-window.9 = s32[8,1]{0,1:T(1,128)S(1)} reduce-window(s32[8,1]{0,1:T(1,128)} %bitcast.18, s32[]{:T(128)} %constant.60.clone.1), window={size=8x1 pad=7_0x0_0}, to_apply=%region_2.3 | reduce-window | flops 56 | bytes 68 | tf_op jit(solution)/shard_map/reduce-window.4
  1.5 0.7 %bitcast_subtract_fusion = s32[8]{0:T(128)S(1)} fusion(s32[8]{0:T(128)} %param.5, s32[8,1]{0,1:T(1,128)S(1)} %reduce-window.9), kind=kLoop, calls=%fused_computation.25 | loop fusion | flops 8 | bytes 96 | tf_op jit(solution)/shard_map/sub | solution.py:20
  2.2 0.8 %select_reduce_fusion = (s32[8]{0:T(128)S(1)}, s32[8]{0:T(128)S(1)}, s32[8]{0:T(128)S(1)}) fusion(s32[8]{0:T(128)S(1)} %bitcast_subtract_fusion, s32[8]{0:T(128)} %param.7, s32[8]{0:T(128)} %param.6, s32[8]{0:T(128)} %param.5), kind=kLoop, calls=%fused_computation.13 | loop fusion | flops 424 | bytes 224 | tf_op jit(solution)/shard_map/reduce_sum | solution.py:12
  3.0 0.1 broadcast_in_dim.78
  3.1 0.1 reshape.167
  3.2 0.1 reshape.165
  3.2 0.1 broadcast_in_dim.72
  3.3 0.1 reshape.161
  3.4 0.1 reshape.166
  3.5 0.1 broadcast_in_dim.75
  3.6 0.1 reshape.162
  3.7 0.2 broadcast_compare_fusion
  3.9 0.0 copy-done
  3.9 1.8 %gather_fusion = bf16[64,2,2304]{2,1,0:T(2,128)(2,1)S(1)} fusion(bf16[32,2,2304]{2,1,0:T(2,128)(2,1)S(1)} %copy-done, s32[1024]{0:T(1024)S(1)} %pad_clamp_fusion), kind=kCustom, calls=%fused_computation | custom fusion | bytes 1179904 | tf_op jit(solution)/shard_map/jit(_take)/gather | solution.py:38
  5.7 1.1 %broadcast_select_fusion.1 = bf16[64,2,2304]{2,1,0:T(2,128)(2,1)S(1)} fusion(pred[64,2304]{1,0:T(8,128)(4,1)S(1)} %broadcast_compare_fusion, bf16[64,2,2304]{2,1,0:T(2,128)(2,1)S(1)} %gather_fusion, pred[64]{0:T(512)(128)(4,1)S(1)} %compare_and_fusion), kind=kLoop, calls=%fused_computation.3 | loop fusion | flops 589824 | bytes 1327168 | tf_op jit(solution)/shard_map/jit(_where)/select_n | solution.py:39
  6.8 23.6 %all_to_all.18 = bf16[64,2,2304]{2,1,0:T(2,128)(2,1)S(1)} all-to-all(bf16[64,2,2304]{2,1,0:T(2,128)(2,1)S(1)} %broadcast_select_fusion.1), channel_id=1, replica_groups=mesh['groups'=2,'seq'=8,'sub'=2] {'seq'}, dimensions={0} | all-to-all | bytes 1179648 | tf_op jit(solution)/shard_map/all_to_all | solution.py:40
  30.4 0.4 %multiply_reduce_fusion = f32[8,2]{1,0:T(8,128)S(1)} fusion(bf16[8,8,2,2304]{3,2,1,0:T(2,128)(2,1)S(1)} %bitcast.15), kind=kLoop, calls=%fused_computation.1 | loop fusion | flops 884720 | bytes 589888 | tf_op jit(solution)/shard_map/reduce_sum | solution.py:41
  30.8 0.2 copy.14
  31.0 0.9 %all_to_all.16 = bf16[8,2,18432]{2,1,0:T(2,128)(2,1)} reshape(bf16[8,2,8,2304]{3,2,1,0:T(8,128)(2,1)S(1)} %bitcast.17) | data formatting | bytes 1179648 | tf_op jit(solution)/shard_map/all_to_all | solution.py:40
  32.0 2.4 %psum.7 = f32[8,2]{1,0:T(8,128)S(1)} all-reduce(f32[8,2]{1,0:T(8,128)S(1)} %multiply_reduce_fusion), channel_id=1, replica_groups=mesh['groups'=2,'seq'=8,'sub'=2] {'sub'}, use_global_device_ids=true, to_apply=%region_5.6 | all-reduce | flops 16 | bytes 128 | tf_op jit(solution)/shard_map/psum | solution.py:42
  34.4 0.6 %copy.10 = f32[2,8]{1,0:T(2,128)} copy(f32[2,8]{0,1:T(8,128)S(1)} %sqrt_bitcast_fusion) | data formatting | bytes 128
  (6 shorter events, 0.1 us)
Async XLA Ops:
  0.6 3.3 %copy-start = (bf16[32,2,2304]{2,1,0:T(2,128)(2,1)S(1)}, bf16[32,2,2304]{2,1,0:T(2,128)(2,1)}, u32[]{:S(2)}) copy-start(bf16[32,2,2304]{2,1,0:T(2,128)(2,1)} %param.4) | copy-start | bytes 884740
where the time goes:
time: 35.3 us; the launch traced here: 35.1 us
  blocking collectives  26 us (74%)
  local copies, waits for them, and re-layouts  4.17 us (12%)
  other arithmetic  4.12 us (12%)
  between operations  0.72 us (2%)
    all_to_all x1, blocking collectives, shards(): lax.all_to_all(packed, 'seq', split_axis=0, concat_axis=2, tiled=True)  23.6 us
    psum x1, blocking collectives, shards(): squares = lax.psum(squares, 'sub')  2.44 us
    gather x1, local copies, waits for them, and re-layouts, shards(): fetched = jnp.take(cache_in, source_rows, axis=0)  1.77 us
    select_n x1, other arithmetic, shards(): packed = jnp.where(kept_mask[:, None, :], fetched, zero_value)  1.14 us
    all_to_all x2, local copies, waits for them, and re-layouts, shards(): lax.all_to_all(packed, 'seq', split_axis=0, concat_axis=2, tiled=True)  1.13 us
    another operation x1, other arithmetic  0.87 us
    reduce_sum x1, other arithmetic, by_device(): return jnp.sum(jnp.where(matches, values[None, :], 0), axis=1)  0.83 us

commit v1 on v0

--- a/solution.py
+++ b/solution.py
@@ -1,18 +1,24 @@
+import functools
+
 import jax
 import jax.numpy as jnp
 from jax import lax
+from jax.experimental import pallas as pl
+from jax.experimental.pallas import tpu as pltpu
 from jax.sharding import PartitionSpec as P
 
 LATENT = 576
 PAGE = 64
 MAXP = 8
+LANES = 128
+MESH = pl.DeviceIdType.MESH
 
 
 def by_device(matches, values):
     return jnp.sum(jnp.where(matches, values[None, :], 0), axis=1)
 
 
-def shards(cache_in, page_counts, tail_tokens, assignment):
+def general(cache_in, page_counts, tail_tokens, assignment):
     seq_count = lax.axis_size("seq")
     own_index = lax.axis_index("seq")
     sub_index = lax.axis_index("sub")
@@ -44,6 +50,170 @@
     return (cache_out, checksum)
 
 
+def far_first(n):
+    return sorted(range(1, n), key=lambda i: -min(i, n - i))
+
+
+def exchange(n, subs, counts, tails, assign, x, out, chk, send, tab, part, parts_in,
+             send_sem, recv_sem, psend_sem, precv_sem, own_sem):
+    me = lax.axis_index("seq")
+    sub = lax.axis_index("sub")
+    pages, layers, piece = x.shape
+    tokens = piece // LATENT
+    own_id = me * subs + sub
+
+    barrier = pltpu.get_barrier_semaphore()
+    for i in range(n):
+        for j in range(subs):
+            if i or j:
+                pl.semaphore_signal(
+                    barrier, inc=1,
+                    device_id={"seq": lax.rem(me + i, n), "sub": lax.rem(sub + j, subs)},
+                    device_id_type=MESH)
+
+    column = lax.broadcasted_iota(jnp.int32, (layers, piece), 1)
+    for f in range(tokens + 1):
+        tab[f] = jnp.where(column < f * LATENT, 1.0, 0.0).astype(x.dtype)
+
+    reqs = counts.shape[0]
+    packed, begin = [], jnp.int32(0)
+    for r in range(reqs):
+        packed.append((begin * 16 + counts[r]) * 128 + tails[r])
+        begin = begin + counts[r]
+    base = (sub * n + me) * tokens
+
+    def gather(i):
+        dest = lax.rem(me + i, n)
+        info = jnp.int32(0)
+        for r in range(reqs):
+            info = info + jnp.where(assign[r] == dest, packed[r], 0)
+        tail = info & 127
+        count = (info >> 7) & 15
+        start = info >> 11
+        for k in range(MAXP):
+            used = k < count
+            row = jnp.where(used, start + k, 0)
+            filled = jnp.where(used, jnp.where(k < count - 1, PAGE, tail), 0)
+            keep = jnp.clip(filled - base, 0, tokens)
+            send[i, k] = x[row] * tab[keep]
+
+    def piece_copy(i):
+        return pltpu.make_async_remote_copy(
+            src_ref=send.at[i],
+            dst_ref=out.at[:, :, pl.ds(pl.multiple_of(me * piece, LANES), piece)],
+            send_sem=send_sem.at[i],
+            recv_sem=recv_sem.at[me],
+            device_id={"seq": lax.rem(me + i, n)},
+            device_id_type=MESH)
+
+    def part_copy(i, j):
+        return pltpu.make_async_remote_copy(
+            src_ref=part.at[i],
+            dst_ref=parts_in.at[own_id],
+            send_sem=psend_sem.at[i * subs + j],
+            recv_sem=precv_sem.at[own_id],
+            device_id={"seq": lax.rem(me + i, n), "sub": lax.rem(sub + j, subs)},
+            device_id_type=MESH)
+
+    order = far_first(n)
+    gather(order[0])
+    gather(order[1])
+    pl.semaphore_wait(barrier, n * subs - 1)
+    started = []
+    for p, i in enumerate(order):
+        if p >= 2:
+            gather(i)
+        if p >= 1:
+            piece_copy(order[p - 1]).start()
+    gather(0)
+    piece_copy(order[-1]).start()
+
+    lane = lax.broadcasted_iota(jnp.int32, (layers, LANES), 1)
+    own_copy = pltpu.make_async_copy(
+        send.at[0], out.at[:, :, pl.ds(pl.multiple_of(me * piece, LANES), piece)], own_sem)
+
+    def squares(i):
+        total = jnp.zeros((layers, LANES), jnp.float32)
+        for k in range(MAXP):
+            v = send[i, k].astype(jnp.float32)
+            s = jnp.sum(v * v, axis=1, keepdims=True)
+            total = jnp.where(lane == k, s, total)
+        return total
+
+    last = None
+    for i in order:
+        part[i] = squares(i)
+        if last is None:
+            own_copy.start()
+        else:
+            for j in range(subs):
+                part_copy(last, j).start()
+        last = i
+    own = squares(0)
+    part[0] = own
+    for j in range(subs):
+        part_copy(last, j).start()
+    parts_in[own_id] = own
+    for j in range(1, subs):
+        part_copy(0, j).start()
+
+    for i in range(n):
+        for j in range(subs):
+            if i or j:
+                src = lax.rem(me + n - i, n) * subs + lax.rem(sub + j, subs)
+                pltpu.make_async_remote_copy(
+                    src_ref=part.at[i],
+                    dst_ref=parts_in.at[src],
+                    send_sem=psend_sem.at[i * subs + j],
+                    recv_sem=precv_sem.at[src],
+                    device_id={"seq": lax.rem(me + i, n), "sub": lax.rem(sub + j, subs)},
+                    device_id_type=MESH).wait()
+    total = jnp.sum(parts_in[...], axis=0)
+    chk[...] = jnp.sqrt(1.0 + total / (PAGE * LATENT))[:, :MAXP]
+    own_copy.wait()
+    for i in order:
+        src = lax.rem(me + n - i, n)
+        pltpu.make_async_remote_copy(
+            src_ref=send.at[i],
+            dst_ref=out.at[:, :, pl.ds(pl.multiple_of(src * piece, LANES), piece)],
+            send_sem=send_sem.at[i],
+            recv_sem=recv_sem.at[src],
+            device_id={"seq": lax.rem(me + i, n)},
+            device_id_type=MESH).wait()
+
+
+def direct(cache_in, page_counts, tail_tokens, assignment):
+    n, subs = lax.axis_size("seq"), lax.axis_size("sub")
+    pages, layers, piece = cache_in.shape
+    vmem = pl.BlockSpec(memory_space=pltpu.VMEM)
+    smem = pl.BlockSpec(memory_space=pltpu.SMEM)
+    return pl.pallas_call(
+        functools.partial(exchange, n, subs),
+        out_shape=(jax.ShapeDtypeStruct((MAXP, layers, piece * n), cache_in.dtype),
+                   jax.ShapeDtypeStruct((layers, MAXP), jnp.float32)),
+        in_specs=[smem, smem, smem, vmem],
+        out_specs=(vmem, vmem),
+        scratch_shapes=[
+            pltpu.VMEM((n, MAXP, layers, piece), cache_in.dtype),
+            pltpu.VMEM((piece // LATENT + 1, layers, piece), cache_in.dtype),
+            pltpu.VMEM((n, layers, LANES), jnp.float32),
+            pltpu.VMEM((n * subs, layers, LANES), jnp.float32),
+            pltpu.SemaphoreType.DMA((n,)),
+            pltpu.SemaphoreType.DMA((n,)),
+            pltpu.SemaphoreType.DMA((n * subs,)),
+            pltpu.SemaphoreType.DMA((n * subs,)),
+            pltpu.SemaphoreType.DMA,
+        ],
+        compiler_params=pltpu.CompilerParams(collective_id=0, has_side_effects=True),
+    )(page_counts, tail_tokens, assignment, cache_in)
+
+
+def shards(cache_in, page_counts, tail_tokens, assignment):
+    piece = cache_in.shape[2]
+    whole_tiles = piece % LANES == 0 and piece % LATENT == 0
+    return (direct if whole_tiles else general)(cache_in, page_counts, tail_tokens, assignment)
+
+
 def solution(mesh):
     placed = (P("groups", None, ("sub", "seq")), P("groups"), P("groups"), P("groups"))
     return jax.shard_map(

time: 35.3 us -> 26.8 us (0.76)
  blocking collectives: 26 us -> 0 us
  Pallas kernels: 0 us -> 23.2 us
  other arithmetic: 4.12 us -> 0 us
  local copies, waits for them, and re-layouts: 4.17 us -> 2.85 us
    all_to_all x1 -> x0, blocking collectives: 23.6 us -> none  [shards(): lax.all_to_all(packed, 'seq', split_axis=0, concat_axis=2, tiled=True)]
    pallas_call x0 -> x1, Pallas kernels: none -> 23.2 us  [direct(): pl.pallas_call(functools.partial(exchange, n, subs), out_shape=(jax.Shape...]
    psum x1 -> x0, blocking collectives: 2.44 us -> none  [shards(): squares = lax.psum(squares, 'sub')]
    unnamed x3 -> x4, local copies, waits for them, and re-layouts: 0.65 us -> 2.85 us
    gather x1 -> x0, local copies, waits for them, and re-layouts: 1.77 us -> none  [shards(): fetched = jnp.take(cache_in, source_rows, axis=0)]
    reduce_sum x2 -> x0, other arithmetic: 1.24 us -> none  [the longest x1 0.83 us: by_device(): return jnp.sum(jnp.where(matches, values[None, :], 0), axis=1)]
    select_n x4 -> x0, other arithmetic: 1.18 us -> none  [the longest x1 1.14 us: shards(): packed = jnp.where(kept_mask[:, None, :], fetched, zero_value)]
    all_to_all x2 -> x0, local copies, waits for them, and re-layouts: 1.13 us -> none  [shards(): lax.all_to_all(packed, 'seq', split_axis=0, concat_axis=2, tiled=True)]
where the time goes in v1:
time: 26.8 us; the launch traced here: 26.7 us
  Pallas kernels  23.2 us (87%)
  local copies, waits for them, and re-layouts  2.85 us (11%)
  between operations  0.65 us (2%)
    pallas_call x1, Pallas kernels, direct(): pl.pallas_call(functools.partial(exchange, n, subs), out_shape=(jax.Shape...  23.2 us
    unnamed x4, local copies, waits for them, and re-layouts  2.85 us

profile of v1, /device:TPU:0, one launch (start us, length us, event | category | flops | bytes accessed | tf_op | source)
XLA Modules:
  0.0 26.7 jit_solution(11533797699764382106)
XLA Ops:
  0.6 23.2 %shard_map.59 = (bf16[8,2,18432]{2,1,0:T(2,128)(2,1)}, f32[2,8]{1,0:T(2,128)}) custom-call(s32[8]{0:T(128)} %counts.1, s32[8]{0:T(128)} %tails.1, s32[8]{0:T(128)} %assign.1, bf16[32,2,2304]{2,1,0:T(2,128)(2,1)} %x.1), custom_call_target="tpu_custom_call" | custom-call | tf_op jit(solution)/shard_map/pallas_call | solution.py:190
  23.8 0.0 copy-start
  23.8 2.3 %copy.8 = bf16[8,2,18432]{2,1,0:T(2,128)(2,1)} copy(bf16[8,2,18432]{2,1,0:T(2,128)(2,1)} %get-tuple-element.4) | data formatting | bytes 1179648
  26.1 0.0 copy-done
  26.1 0.6 %copy.9 = f32[2,8]{1,0:T(2,128)} copy(f32[2,8]{1,0:T(2,128)S(1)} %copy-done) | data formatting | bytes 128
Async XLA Ops:
  23.8 2.3 %copy-start = (f32[2,8]{1,0:T(2,128)S(1)}, f32[2,8]{1,0:T(2,128)}, u32[]{:S(2)}) copy-start(f32[2,8]{1,0:T(2,128)} %get-tuple-element.5) | copy-start | bytes 196

commit v2 on v0

--- a/solution.py
+++ b/solution.py
@@ -1,18 +1,25 @@
+import functools
+
 import jax
 import jax.numpy as jnp
 from jax import lax
+from jax.experimental import pallas as pl
+from jax.experimental.pallas import tpu as pltpu
 from jax.sharding import PartitionSpec as P
 
 LATENT = 576
 PAGE = 64
 MAXP = 8
+LANES = 128
+ROW_CHIPS = 2
+MESH = pl.DeviceIdType.MESH
 
 
 def by_device(matches, values):
     return jnp.sum(jnp.where(matches, values[None, :], 0), axis=1)
 
 
-def shards(cache_in, page_counts, tail_tokens, assignment):
+def general(cache_in, page_counts, tail_tokens, assignment):
     seq_count = lax.axis_size("seq")
     own_index = lax.axis_index("seq")
     sub_index = lax.axis_index("sub")
@@ -44,6 +51,180 @@
     return (cache_out, checksum)
 
 
+def exchange(n, subs, counts_in, tails_in, assign_in, x_in, out, chk, send, tab, part, parts_in,
+             send_sem, recv_sem, psend_sem, precv_sem, ready_sem, own_sem, in_sem,
+             x, counts, tails, assign):
+    me = lax.axis_index("seq")
+    sub = lax.axis_index("sub")
+    pages, layers, piece = x.shape
+    tokens = piece // LATENT
+    own_id = me * subs + sub
+    line = n // ROW_CHIPS
+    z, col = me // ROW_CHIPS, me % ROW_CHIPS
+    steps = [(dz, dx) for dx in range(ROW_CHIPS) for dz in range(1 - line, line) if dz or dx]
+    steps.sort(key=lambda step: (-abs(step[0]), -step[1]))
+
+    def inside(step):
+        return jnp.logical_and(z + step[0] >= 0, z + step[0] < line)
+
+    def peer(step):
+        return (z + step[0]) * ROW_CHIPS + (col + step[1]) % ROW_CHIPS
+
+    def device(other):
+        return {"seq": other // subs, "sub": other % subs}
+
+    everyone = range(n * subs)
+    arrivals = [pltpu.make_async_copy(a, b, in_sem.at[k]) for k, (a, b) in enumerate(
+        ((counts_in, counts), (tails_in, tails), (assign_in, assign), (x_in, x)))]
+    for copy in arrivals:
+        copy.start()
+    barrier = pltpu.get_barrier_semaphore()
+    for other in everyone:
+        @pl.when(other > own_id)
+        def _():
+            pl.semaphore_signal(
+                barrier, inc=1, device_id=device(other), device_id_type=MESH)
+
+    column = lax.broadcasted_iota(jnp.int32, (layers, piece), 1)
+    for f in range(tokens + 1):
+        tab[f] = jnp.where(column < f * LATENT, 1.0, 0.0).astype(x.dtype)
+
+    for copy in arrivals:
+        copy.wait()
+    reqs = counts.shape[0]
+    packed, begin = [], jnp.int32(0)
+    for r in range(reqs):
+        packed.append((begin * 16 + counts[r]) * 128 + tails[r])
+        begin = begin + counts[r]
+    base = (sub * n + me) * tokens
+
+    for dest in range(n):
+        info = jnp.int32(0)
+        for r in range(reqs):
+            info = info + jnp.where(assign[r] == dest, packed[r], 0)
+        tail = info & 127
+        count = (info >> 7) & 15
+        start = info >> 11
+        for k in range(MAXP):
+            used = k < count
+            row = jnp.where(used, start + k, 0)
+            filled = jnp.where(used, jnp.where(k < count - 1, PAGE, tail), 0)
+            keep = jnp.clip(filled - base, 0, tokens)
+            send[dest, k] = x[row] * tab[keep]
+
+    def columns(source):
+        return out.at[:, :, pl.ds(pl.multiple_of(source * piece, LANES), piece)]
+
+    def piece_copy(dest, source):
+        return pltpu.make_async_remote_copy(
+            src_ref=send.at[dest],
+            dst_ref=columns(source),
+            send_sem=send_sem.at[dest],
+            recv_sem=recv_sem.at[source],
+            device_id={"seq": dest},
+            device_id_type=MESH)
+
+    def part_copy(i, j, source):
+        dest = (me + i) % n
+        return pltpu.make_async_remote_copy(
+            src_ref=part.at[dest],
+            dst_ref=parts_in.at[source],
+            send_sem=psend_sem.at[i * subs + j],
+            recv_sem=precv_sem.at[source],
+            device_id={"seq": dest, "sub": (sub + j) % subs},
+            device_id_type=MESH)
+
+    own_copy = pltpu.make_async_copy(send.at[me], columns(me), own_sem)
+
+    @pl.when(own_id > 0)
+    def _():
+        pl.semaphore_wait(barrier, own_id)
+
+    for other in everyone:
+        @pl.when(other < own_id)
+        def _():
+            pl.semaphore_signal(
+                ready_sem.at[own_id], inc=1, device_id=device(other), device_id_type=MESH)
+    for step in steps:
+        @pl.when(jnp.logical_and(inside(step), peer(step) < me))
+        def _():
+            piece_copy(peer(step), me).start()
+    own_copy.start()
+    for dest in range(1, n):
+        @pl.when(dest > me)
+        def _():
+            pl.semaphore_wait(ready_sem.at[dest * subs + sub], 1)
+            piece_copy(dest, me).start()
+
+    lane = lax.broadcasted_iota(jnp.int32, (layers, LANES), 1)
+    for dest in range(n):
+        total = jnp.zeros((layers, LANES), jnp.float32)
+        for k in range(MAXP):
+            v = send[dest, k].astype(jnp.float32)
+            s = jnp.sum(v * v, axis=1, keepdims=True)
+            total = jnp.where(lane == k, s, total)
+        part[dest] = total
+    parts_in[own_id] = part[me]
+    for other in everyone:
+        @pl.when(jnp.logical_and(other > own_id, other % subs != sub))
+        def _():
+            pl.semaphore_wait(ready_sem.at[other], 1)
+    others = [(i, j) for i in range(n) for j in range(subs) if i or j]
+    for i, j in others:
+        part_copy(i, j, own_id).start()
+
+    own_copy.wait()
+    for i in range(1, n):
+        pltpu.make_async_remote_copy(
+            src_ref=send.at[(me + i) % n],
+            dst_ref=columns((me + n - i) % n),
+            send_sem=send_sem.at[(me + i) % n],
+            recv_sem=recv_sem.at[(me + n - i) % n],
+            device_id={"seq": (me + i) % n},
+            device_id_type=MESH).wait()
+    for i, j in others:
+        part_copy(i, j, (me + n - i) % n * subs + (sub + subs - j) % subs).wait()
+    total = jnp.sum(parts_in[...], axis=0)
+    chk[...] = jnp.sqrt(1.0 + total / (PAGE * LATENT))[:, :MAXP]
+
+
+def direct(cache_in, page_counts, tail_tokens, assignment):
+    n, subs = lax.axis_size("seq"), lax.axis_size("sub")
+    pages, layers, piece = cache_in.shape
+    vmem = pl.BlockSpec(memory_space=pltpu.VMEM)
+    return pl.pallas_call(
+        functools.partial(exchange, n, subs),
+        out_shape=(pltpu.VMEM((MAXP, layers, piece * n), cache_in.dtype),
+                   pltpu.VMEM((layers, MAXP), jnp.float32)),
+        in_specs=[pl.BlockSpec(memory_space=pl.ANY)] * 4,
+        out_specs=(vmem, vmem),
+        scratch_shapes=[
+            pltpu.VMEM((n, MAXP, layers, piece), cache_in.dtype),
+            pltpu.VMEM((piece // LATENT + 1, layers, piece), cache_in.dtype),
+            pltpu.VMEM((n, layers, LANES), jnp.float32),
+            pltpu.VMEM((n * subs, layers, LANES), jnp.float32),
+            pltpu.SemaphoreType.DMA((n,)),
+            pltpu.SemaphoreType.DMA((n,)),
+            pltpu.SemaphoreType.DMA((n * subs,)),
+            pltpu.SemaphoreType.DMA((n * subs,)),
+            pltpu.SemaphoreType.REGULAR((n * subs,)),
+            pltpu.SemaphoreType.DMA,
+            pltpu.SemaphoreType.DMA((4,)),
+            pltpu.VMEM(cache_in.shape, cache_in.dtype),
+            pltpu.SMEM(page_counts.shape, jnp.int32),
+            pltpu.SMEM(page_counts.shape, jnp.int32),
+            pltpu.SMEM(page_counts.shape, jnp.int32),
+        ],
+        compiler_params=pltpu.CompilerParams(collective_id=0, has_side_effects=True),
+    )(page_counts, tail_tokens, assignment, cache_in)
+
+
+def shards(cache_in, page_counts, tail_tokens, assignment):
+    piece = cache_in.shape[2]
+    whole_tiles = piece % LANES == 0 and piece % LATENT == 0 and lax.axis_size("seq") % ROW_CHIPS == 0
+    return (direct if whole_tiles else general)(cache_in, page_counts, tail_tokens, assignment)
+
+
 def solution(mesh):
     placed = (P("groups", None, ("sub", "seq")), P("groups"), P("groups"), P("groups"))
     return jax.shard_map(

time: 35.3 us -> 23.1 us (0.65)
  blocking collectives: 26 us -> 0 us
  Pallas kernels: 0 us -> 21 us
  other arithmetic: 4.12 us -> 0 us
  local copies, waits for them, and re-layouts: 4.17 us -> 1.38 us
    all_to_all x1 -> x0, blocking collectives: 23.6 us -> none  [shards(): lax.all_to_all(packed, 'seq', split_axis=0, concat_axis=2, tiled=True)]
    pallas_call x0 -> x1, Pallas kernels: none -> 21 us  [direct(): pl.pallas_call(functools.partial(exchange, n, subs), out_shape=(pltpu.VME...]
    psum x1 -> x0, blocking collectives: 2.44 us -> none  [shards(): squares = lax.psum(squares, 'sub')]
    gather x1 -> x0, local copies, waits for them, and re-layouts: 1.77 us -> none  [shards(): fetched = jnp.take(cache_in, source_rows, axis=0)]
    reduce_sum x2 -> x0, other arithmetic: 1.24 us -> none  [the longest x1 0.83 us: by_device(): return jnp.sum(jnp.where(matches, values[None, :], 0), axis=1)]
    select_n x4 -> x0, other arithmetic: 1.18 us -> none  [the longest x1 1.14 us: shards(): packed = jnp.where(kept_mask[:, None, :], fetched, zero_value)]
    all_to_all x2 -> x0, local copies, waits for them, and re-layouts: 1.13 us -> none  [shards(): lax.all_to_all(packed, 'seq', split_axis=0, concat_axis=2, tiled=True)]
    another operation x1 -> x0, other arithmetic: 0.87 us -> none
where the time goes in v2:
time: 23.1 us; the launch traced here: 23 us
  Pallas kernels  21 us (91%)
  local copies, waits for them, and re-layouts  1.38 us (6%)
  between operations  0.64 us (3%)
    pallas_call x1, Pallas kernels, direct(): pl.pallas_call(functools.partial(exchange, n, subs), out_shape=(pltpu.VME...  21 us
    unnamed x2, local copies, waits for them, and re-layouts  1.38 us

profile of v2, /device:TPU:0, one launch (start us, length us, event | category | flops | bytes accessed | tf_op | source)
XLA Modules:
  0.0 23.0 jit_solution(8340306939790457553)
XLA Ops:
  0.6 21.0 %shard_map.59 = (bf16[8,2,18432]{2,1,0:T(2,128)(2,1)S(1)}, f32[2,8]{1,0:T(2,128)S(1)}) custom-call(s32[8]{0:T(128)} %counts_in.1, s32[8]{0:T(128)} %tails_in.1, s32[8]{0:T(128)} %assign_in.1, bf16[32,2,2304]{2,1,0:T(2,128)(2,1)} %x_in.1), custom_call_target="tpu_custom_call" | custom-call | tf_op jit(solution)/shard_map/pallas_call | solution.py:195
  21.6 0.8 %copy.8 = bf16[8,2,18432]{2,1,0:T(2,128)(2,1)} copy(bf16[8,2,18432]{2,1,0:T(2,128)(2,1)S(1)} %get-tuple-element.2) | data formatting | bytes 1179648
  22.4 0.6 %copy.9 = f32[2,8]{1,0:T(2,128)} copy(f32[2,8]{1,0:T(2,128)S(1)} %get-tuple-element.3) | data formatting | bytes 128

commit v3 on v2

--- a/solution.py
+++ b/solution.py
@@ -188,11 +188,20 @@
     chk[...] = jnp.sqrt(1.0 + total / (PAGE * LATENT))[:, :MAXP]
 
 
+def place(pages_in, sums_in, pages, sums, sem):
+    copies = [pltpu.make_async_copy(a, b, sem.at[k]) for k, (a, b) in enumerate(
+        ((pages_in, pages), (sums_in, sums)))]
+    for copy in copies:
+        copy.start()
+    for copy in copies:
+        copy.wait()
+
+
 def direct(cache_in, page_counts, tail_tokens, assignment):
     n, subs = lax.axis_size("seq"), lax.axis_size("sub")
     pages, layers, piece = cache_in.shape
     vmem = pl.BlockSpec(memory_space=pltpu.VMEM)
-    return pl.pallas_call(
+    landed = pl.pallas_call(
         functools.partial(exchange, n, subs),
         out_shape=(pltpu.VMEM((MAXP, layers, piece * n), cache_in.dtype),
                    pltpu.VMEM((layers, MAXP), jnp.float32)),
@@ -217,6 +226,13 @@
         ],
         compiler_params=pltpu.CompilerParams(collective_id=0, has_side_effects=True),
     )(page_counts, tail_tokens, assignment, cache_in)
+    return pl.pallas_call(
+        place,
+        out_shape=tuple(jax.ShapeDtypeStruct(a.shape, a.dtype) for a in landed),
+        in_specs=[vmem] * 2,
+        out_specs=(pl.BlockSpec(memory_space=pltpu.HBM),) * 2,
+        scratch_shapes=[pltpu.SemaphoreType.DMA((2,))],
+    )(*(pltpu.with_memory_space_constraint(a, pltpu.VMEM) for a in landed))
 
 
 def shards(cache_in, page_counts, tail_tokens, assignment):

time: 23.1 us -> 22.6 us (0.978)
  local copies, waits for them, and re-layouts: 1.38 us -> 0 us
  Pallas kernels: 21 us -> 21.8 us
    unnamed x2 -> x0, local copies, waits for them, and re-layouts: 1.38 us -> none
    pallas_call x0 -> x1, Pallas kernels: none -> 0.84 us  [direct(): pl.pallas_call(place, out_shape=tuple((jax.ShapeDtypeStruct(a.shape, a.dt...]
where the time goes in v3:
time: 22.6 us; the launch traced here: 22.4 us
  Pallas kernels  21.8 us (96%)
  between operations  0.64 us (3%)
    pallas_call x1, Pallas kernels, direct(): pl.pallas_call(functools.partial(exchange, n, subs), out_shape=(pltpu.VME...  21 us
    pallas_call x1, Pallas kernels, direct(): pl.pallas_call(place, out_shape=tuple((jax.ShapeDtypeStruct(a.shape, a.dt...  0.84 us

profile of v3, /device:TPU:0, one launch (start us, length us, event | category | flops | bytes accessed | tf_op | source)
XLA Modules:
  0.0 22.4 jit_solution(3438238470118986704)
XLA Ops:
  0.6 21.0 %shard_map.59 = (bf16[8,2,18432]{2,1,0:T(2,128)(2,1)S(1)}, f32[2,8]{1,0:T(2,128)S(1)}) custom-call(s32[8]{0:T(128)} %counts_in.1, s32[8]{0:T(128)} %tails_in.1, s32[8]{0:T(128)} %assign_in.1, bf16[32,2,2304]{2,1,0:T(2,128)(2,1)} %x_in.1), custom_call_target="tpu_custom_call" | custom-call | tf_op jit(solution)/shard_map/pallas_call | solution.py:204
  21.6 0.8 %shard_map.60 = (bf16[8,2,18432]{2,1,0:T(2,128)(2,1)}, f32[2,8]{1,0:T(2,128)}) custom-call(bf16[8,2,18432]{2,1,0:T(2,128)(2,1)S(1)} %get-tuple-element.4.pages_in, f32[2,8]{1,0:T(2,128)S(1)} %get-tuple-element.5.sums_in), custom_call_target="tpu_custom_call" | custom-call | tf_op jit(solution)/shard_map/pallas_call | solution.py:229
